TPU v7x, 128 devices: a whole 4x4x4 slice. The times are simulated.
128 devices in a mesh: bank: 4 (over z), zero: 32 (over y, x, core).
Axes of the slice: x: 4, y: 4, z: 4, core: 2. Of those that a mesh axis runs over, the one named last changes fastest.
Arguments:
- w_gate: float32 [128, 2048, 768], P('bank', 'zero'), may hold values from -0.25 to 0.25
- w_up: float32 [128, 2048, 768], P('bank', 'zero'), may hold values from -0.25 to 0.25
- router_weight: float32 [2048, 128], P('zero', 'bank'), may hold values from -0.125 to 0.125
- router_gain: float32 [2048], P('zero'), may hold values from 0.25 to 1.75
Outputs:
- serve_gate: bfloat16 [128, 2048, 768], P('bank', None, 'zero')
- serve_up: bfloat16 [128, 2048, 768], P('bank', None, 'zero')
- scale_gate: float32 [128, 768], P('bank', 'zero')
- scale_up: float32 [128, 768], P('bank', 'zero')
- serve_router: bfloat16 [2048, 128], replicated
All inputs are finite; a program needn't handle non-finite values.
Results may differ from a plain program's by a relative error of at most 0.001.
Values may be sent and summed in bfloat16 or wider, within the bound.
A program may use at most 128 MiB of HBM per device.

v0:
```python
import jax
import jax.numpy as jnp
from jax import lax
from jax.sharding import PartitionSpec as P


def over_pieces(value, axis):
    return lax.all_gather(value, axis).sum(0)


def in_one_piece(arrays, axis, split_dim, concat_dim, along):
    both = jnp.concatenate(arrays, axis=along)
    filled, at, outs = (
        lax.all_to_all(both, axis, split_axis=split_dim, concat_axis=concat_dim, tiled=True),
        0,
        [],
    )
    for a in arrays:
        outs.append(lax.slice_in_dim(filled, at, at + a.shape[along], axis=along))
        at += a.shape[along]
    return tuple(outs)


def from_everyone(value, axis):
    count = lax.axis_size(axis)
    return lax.all_to_all(
        jnp.broadcast_to(value[None], (count, *value.shape)), axis, 0, 0, tiled=True
    )


def in_order(parts, dim):
    shape = list(parts.shape[1:])
    shape[dim] *= parts.shape[0]
    return jnp.moveaxis(parts, 0, dim).reshape(shape)


def gather_directly(value, axis, dim):
    parts = from_everyone(value, axis)
    return in_order(parts, dim)


def shards(w_gate, w_up, router_weight, router_gain):
    total_gate, total_up = (
        over_pieces(jnp.sum(w_gate * w_gate, axis=1), "zero"),
        over_pieces(jnp.sum(w_up * w_up, axis=1), "zero"),
    )
    scale_gate = jnp.sqrt(total_gate)
    scale_up = jnp.sqrt(total_up)
    narrow_gate, narrow_up = (
        (w_gate / jnp.expand_dims(scale_gate, 1)).astype(jnp.bfloat16),
        (w_up / jnp.expand_dims(scale_up, 1)).astype(jnp.bfloat16),
    )
    serve_gate, serve_up = in_one_piece((narrow_gate, narrow_up), "zero", 2, 1, 0)
    scale_gate = lax.dynamic_slice_in_dim(
        scale_gate, lax.axis_index("zero") * serve_gate.shape[2], serve_gate.shape[2], axis=1
    )
    scale_up = lax.dynamic_slice_in_dim(
        scale_up, lax.axis_index("zero") * serve_up.shape[2], serve_up.shape[2], axis=1
    )
    part_router = (router_weight * router_gain[:, None]).astype(jnp.bfloat16)
    row_router = gather_directly(part_router, "zero", 0)
    serve_router = gather_directly(row_router, "bank", 1)
    return (serve_gate, serve_up, scale_gate, scale_up, serve_router)


def solution(mesh):
    placed = (P("bank", "zero", None), P("bank", "zero", None), P("zero", "bank"), P("zero"))
    return jax.shard_map(
        shards,
        mesh=mesh,
        in_specs=placed,
        out_specs=(
            P("bank", None, "zero"),
            P("bank", None, "zero"),
            P("bank", "zero"),
            P("bank", "zero"),
            P(),
        ),
        check_vma=False,
    )
```

profile of v0, /device:TPU:1, one launch (start us, length us, event | category | flops | bytes accessed | tf_op | source)
XLA Modules:
  0.0 302.5 jit_solution(14768437558272793560)
XLA Ops:
  7.2 0.0 copy-start
  7.2 0.0 copy-start.1
  7.2 0.0 all-gather.5.cloned.1.call-start
  7.2 4.1 %multiply_reduce_fusion.1 = f32[32,768]{1,0:T(8,128)} fusion(f32[32,64,768]{2,1,0:T(8,128)} %param.4), kind=kLoop, calls=%fused_computation.4 | loop fusion | flops 3121152 | bytes 6389760 | tf_op jit(solution)/shard_map/reduce_sum | solution.py:44
  11.4 0.0 all-gather.5.cloned.1.call-update
  11.4 0.0 all-gather.7.cloned.1.call-start
  11.5 4.1 %multiply_reduce_fusion = f32[32,768]{1,0:T(8,128)} fusion(f32[32,64,768]{2,1,0:T(8,128)} %param.5), kind=kLoop, calls=%fused_computation.3 | loop fusion | flops 3121152 | bytes 6389760 | tf_op jit(solution)/shard_map/reduce_sum | solution.py:45
  15.6 0.0 all-gather.7.cloned.1.call-update
  15.6 0.0 copy-done
  15.6 0.0 copy-done.1
  15.7 0.8 reshape.29
  16.6 8.6 %all-to-all-start.1 = ((bf16[32,2,1024]{2,1,0:T(2,128)(2,1)}), bf16[32,2,1024]{2,1,0:T(2,128)(2,1)S(1)}, u32[]{:S(2)}, u32[]{:S(2)}) async-start(bf16[32,2,1024]{2,1,0:T(2,128)(2,1)} %reshape.29), calls=%async_computation.1 | async-start | bytes 262144 | tf_op jit(solution)/shard_map/all_to_all | solution.py:26
  25.1 12.7 %copy.39 = f32[32,64,768]{1,0,2:T(8,128)} copy(f32[32,64,768]{2,1,0:T(8,128)} %param.4) | data formatting | bytes 12582912 | tf_op args[0]
  37.8 12.7 %copy.41 = f32[32,64,768]{1,0,2:T(8,128)} copy(f32[32,64,768]{2,1,0:T(8,128)} %param.5) | data formatting | bytes 12582912 | tf_op args[1]
  50.5 0.0 all-to-all-done.1
  50.5 0.2 reshape.30
  50.7 0.1 copy.45
  50.8 0.3 broadcast_in_dim.7
  51.1 0.9 broadcast_in_dim.8
  52.0 5.0 %all-to-all-start.2 = ((bf16[4,2048,32]{1,2,0:T(8,128)(2,1)}), bf16[4,2048,32]{1,2,0:T(8,128)(2,1)S(1)}, u32[]{:S(2)}, u32[]{:S(2)}) async-start(bf16[4,2048,32]{1,2,0:T(8,128)(2,1)} %broadcast_in_dim.8), calls=%async_computation.2 | async-start | bytes 1048576 | tf_op jit(solution)/shard_map/all_to_all | solution.py:26
  57.0 2.8 all-gather.5.cloned.1.call-done
  59.8 2.0 reduce_sum.37
  61.9 44.9 %all-gather.7.cloned.1.call-done = f32[1024,768]{1,0:T(8,128)} async-done(((f32[32,768]{1,0:T(8,128)}), f32[1024,768]{1,0:T(8,128)}) %all-gather.7.cloned.1.call-update) | async-done | bytes 3145744 | tf_op jit(solution)/shard_map/all_gather | solution.py:8
  106.8 2.0 reduce_sum.39
  108.9 0.2 copy.38
  109.0 0.2 copy.40
  109.2 9.4 %divide_convert_fusion = (bf16[32,64,768]{1,0,2:T(8,128)(2,1)S(1)}, bf16[32,64,768]{1,0,2:T(8,128)(2,1)S(1)}) fusion(f32[32,64,768]{1,0,2:T(8,128)} %copy.41, f32[32,768]{0,1:T(8,128)S(1)} %copy.40, f32[32,64,768]{1,0,2:T(8,128)} %copy.39, f32[32,768]{0,1:T(8,128)S(1)} %copy.38), kind=kLoop, calls=%fused_computation.1 | loop fusion | flops 6291456 | bytes 19070976 | tf_op jit(solution)/shard_map/convert_element_type | solution.py:51
  118.6 6.5 %fusion.1 = bf16[768,64,64]{2,1,0:T(8,128)(2,1)} fusion(bf16[32,64,768]{1,0,2:T(8,128)(2,1)S(1)} %get-tuple-element.32, bf16[32,64,768]{1,0,2:T(8,128)(2,1)S(1)} %get-tuple-element.33), kind=kLoop, calls=%fused_computation.9 | loop fusion | flops 12582912 | bytes 12582912
  125.0 24.2 %reshape.27 = bf16[32,2,49152]{2,1,0:T(2,128)(2,1)} reshape(bf16[768,64,64]{2,1,0:T(8,128)(2,1)} %fusion.1) | data formatting | bytes 12582912
  149.2 0.0 all-to-all-done.2
  149.2 5.4 %all-to-all-start = ((bf16[32,2,49152]{2,1,0:T(2,128)(2,1)}), bf16[32,2,49152]{2,1,0:T(2,128)(2,1)}, u32[]{:S(2)}, u32[]{:S(2)}) async-start(bf16[32,2,49152]{2,1,0:T(2,128)(2,1)} %reshape.27), calls=%async_computation | async-start | bytes 12582912 | tf_op jit(solution)/shard_map/all_to_all | solution.py:14
  154.6 1.0 copy.48
  155.6 0.1 constant_dynamic-slice_fusion
  155.7 0.7 copy.46
  156.4 0.7 copy.47
  157.0 70.8 %all-to-all-done = bf16[32,2,49152]{2,1,0:T(2,128)(2,1)} async-done(((bf16[32,2,49152]{2,1,0:T(2,128)(2,1)}), bf16[32,2,49152]{2,1,0:T(2,128)(2,1)}, u32[]{:S(2)}, u32[]{:S(2)}) %all-to-all-start) | async-done | bytes 6291488 | tf_op jit(solution)/shard_map/all_to_all | solution.py:14
  227.9 23.5 %reshape.28 = bf16[768,64,64]{2,1,0:T(8,128)(2,1)} reshape(bf16[32,2,49152]{2,1,0:T(2,128)(2,1)} %all-to-all-done) | data formatting | bytes 12582912
  251.4 9.5 %copy.42 = bf16[64,64,768]{1,2,0:T(8,128)(2,1)S(1)} copy(bf16[64,64,768]{1,0,2:T(8,128)(2,1)} %bitcast.25) | data formatting | bytes 12582912 | tf_op jit(solution)/shard_map/all_to_all | solution.py:14
  260.9 4.3 %fusion = (bf16[32,32,64,24]{2,3,1,0:T(8,128)(2,1)}, bf16[32,32,64,24]{2,3,1,0:T(8,128)(2,1)S(1)}) fusion(bf16[64,32,64,24]{2,3,1,0:T(8,128)(2,1)S(1)} %bitcast.24), kind=kLoop, calls=%fused_computation.8 | loop fusion | bytes 12582912 | tf_op jit(solution)/shard_map/slice | solution.py:19
  265.2 4.1 %copy.43 = bf16[32,32,64,24]{2,1,3,0:T(8,128)(2,1)} copy(bf16[32,32,64,24]{2,3,1,0:T(8,128)(2,1)S(1)} %get-tuple-element.31) | data formatting | bytes 6291456 | tf_op jit(solution)/shard_map/slice | solution.py:19
  269.3 9.7 %slice.13 = bf16[32,2048,24]{1,2,0:T(8,128)(2,1)} reshape(bf16[32,32,64,24]{2,1,3,0:T(8,128)(2,1)} %copy.43) | data formatting | bytes 6291456 | tf_op jit(solution)/shard_map/slice | solution.py:19
  279.0 6.9 %copy.44 = bf16[32,32,64,24]{2,1,3,0:T(8,128)(2,1)} copy(bf16[32,32,64,24]{2,3,1,0:T(8,128)(2,1)} %get-tuple-element.30) | data formatting | bytes 6291456 | tf_op jit(solution)/shard_map/slice | solution.py:19
  285.9 9.7 %slice.15 = bf16[32,2048,24]{1,2,0:T(8,128)(2,1)} reshape(bf16[32,32,64,24]{2,1,3,0:T(8,128)(2,1)} %copy.44) | data formatting | bytes 6291456 | tf_op jit(solution)/shard_map/slice | solution.py:19
  (4 shorter events, 0.1 us)
Async XLA Ops:
  7.2 8.5 %copy-start = (f32[64,32]{0,1:T(8,128)S(1)}, f32[64,32]{0,1:T(8,128)}, u32[]{:S(2)}) copy-start(f32[64,32]{0,1:T(8,128)} %param.6) | copy-start | bytes 24580
  7.2 8.5 %copy-start.1 = (f32[64]{0:T(128)S(1)}, f32[64]{0:T(128)}, u32[]{:S(2)}) copy-start(f32[64]{0:T(128)} %param.7) | copy-start | bytes 772
  7.2 52.6 %all-gather.5.cloned.1.call-start = ((), (), s32[]{:S(2)}) async-start(), calls=%async_computation.3 | async-start | bytes 3244032 | tf_op jit(solution)/shard_map/all_gather | solution.py:8
  11.4 95.4 %all-gather.7.cloned.1.call-start = ((), (), s32[]{:S(2)}) async-start(), calls=%async_computation.4 | async-start | bytes 3244032 | tf_op jit(solution)/shard_map/all_gather | solution.py:8
  16.6 33.9 %all-to-all-start.1 = ((bf16[32,2,1024]{2,1,0:T(2,128)(2,1)}), bf16[32,2,1024]{2,1,0:T(2,128)(2,1)S(1)}, u32[]{:S(2)}, u32[]{:S(2)}) async-start(bf16[32,2,1024]{2,1,0:T(2,128)(2,1)} %reshape.29), calls=%async_computation.1 | async-start | bytes 262144 | tf_op jit(solution)/shard_map/all_to_all | solution.py:26
  52.0 97.3 %all-to-all-start.2 = ((bf16[4,2048,32]{1,2,0:T(8,128)(2,1)}), bf16[4,2048,32]{1,2,0:T(8,128)(2,1)S(1)}, u32[]{:S(2)}, u32[]{:S(2)}) async-start(bf16[4,2048,32]{1,2,0:T(8,128)(2,1)} %broadcast_in_dim.8), calls=%async_computation.2 | async-start | bytes 1048576 | tf_op jit(solution)/shard_map/all_to_all | solution.py:26
  149.2 78.6 %all-to-all-start = ((bf16[32,2,49152]{2,1,0:T(2,128)(2,1)}), bf16[32,2,49152]{2,1,0:T(2,128)(2,1)}, u32[]{:S(2)}, u32[]{:S(2)}) async-start(bf16[32,2,49152]{2,1,0:T(2,128)(2,1)} %reshape.27), calls=%async_computation | async-start | bytes 12582912 | tf_op jit(solution)/shard_map/all_to_all | solution.py:14
Sparse Core Ops, SparseCore 0:
  11.5 48.2 all-gather.4
  62.7 44.0 all-gather.6
where the time goes:
time: 309 us; the launch traced here: 302 us
  local copies, waits for them, and re-layouts  122 us (39%)
  waiting for transfers between devices  119 us (39%)
  other arithmetic  28.2 us (9%)
  starting transfers between devices  19 us (6%)
  between operations  14.2 us (5%)
    unnamed x14, local copies, waits for them, and re-layouts  76.5 us
    all_to_all x1, waiting for transfers between devices, in_one_piece(): lax.all_to_all(both, axis, split_axis=split_dim, concat_axis=concat_dim,...  70.8 us
    all_gather x2, waiting for transfers between devices, over_pieces(): return lax.all_gather(value, axis).sum(0)  47.7 us
    slice x5, local copies, waits for them, and re-layouts, in_one_piece(): outs.append(lax.slice_in_dim(filled, at, at + a.shape[along], axis=along))  34.8 us
    all_to_all x2, starting transfers between devices, from_everyone(): lax.all_to_all(jnp.broadcast_to(value[None], (count, *value.shape)), axis...  13.6 us
    all_to_all x1, local copies, waits for them, and re-layouts, in_one_piece(): lax.all_to_all(both, axis, split_axis=split_dim, concat_axis=concat_dim,...  9.5 us
    convert_element_type x1, other arithmetic, shards(): (w_up / jnp.expand_dims(scale_up, 1)).astype(jnp.bfloat16)  9.38 us
    unnamed x1, other arithmetic  6.45 us
  transfers between devices with their start and end apart: 5, of which 3 were waited for; matrix products, arithmetic and copies ran while one was open for 26% of the time, Pallas kernels for 0%

commit v1 on v0

v1 whole, which is shorter than its diff:
```python
import functools

import jax
import jax.numpy as jnp
from jax import lax
from jax.experimental import pallas as pl
from jax.experimental.pallas import tpu as pltpu
from jax.sharding import PartitionSpec as P

MESH = pl.DeviceIdType.MESH
Z = 32
LANES = 128


def plane_peer(me, k):
    k = (11 * k) % 32
    dy, dx, dc = k // 8, (k // 2) % 4, k % 2
    y, x, c = me // 8, (me // 2) % 4, me % 2
    return (((y + dy) % 4) * 4 + (x + dx) % 4) * 2 + (c + dc) % 2


def exchange(
    experts, rows, cols, chunk,
    gate_hbm, up_hbm, router_ref, gain_ref,
    out_gate, out_up, out_sgate, out_sup, out_router,
    held, sums, parts, scales, inverse, scales_t, send, recv, router_part, router_got,
    load_sem, rs_send, rs_recv, ag_send, ag_recv, bulk_send, bulk_recv,
    rt_send, rt_recv, rx_send, rx_recv,
):
    bank = lax.axis_index("bank")
    me = lax.axis_index("zero")
    core = me % 2
    blocks = cols // LANES
    own = cols // Z
    pairs = experts // 2
    half = blocks // 2
    weights = (gate_hbm, up_hbm)
    loads = 4
    step = experts // loads

    barrier = pltpu.get_barrier_semaphore()

    def greet(k, _):
        pl.semaphore_signal(barrier, inc=1, device_id={"zero": plane_peer(me, k)}, device_id_type=MESH)
        return 0

    lax.fori_loop(1, Z, greet, 0)
    for dz in range(1, 4):
        for dc in range(2):
            pl.semaphore_signal(
                barrier, inc=1,
                device_id={"bank": (bank + dz) % 4, "zero": (me // 2) * 2 + (core + dc) % 2},
                device_id_type=MESH,
            )

    copies = []
    for w in range(2):
        for q in range(loads):
            at = pl.ds(q * step, step)
            copy = pltpu.make_async_copy(weights[w].at[at], held.at[w, at], load_sem.at[w * loads + q])
            copy.start()
            copies.append(copy)

    low = router_ref[:16, :] * gain_ref[...]
    high = router_ref[16:, :] * gain_ref[...]
    first = jnp.where(core == 0, low, high)
    second = jnp.where(core == 0, high, low)
    packed = jnp.concatenate([first, second], axis=1).astype(jnp.bfloat16)
    router_part[me // 2] = packed

    def sums_of(w, q):
        copies[w * loads + q].wait()

        def body(e, _):
            for b in range(blocks):
                x = held[w, e, :, b * LANES:(b + 1) * LANES]
                sums[w, e, b:b + 1, :] = jnp.sum(x * x, axis=0, keepdims=True)
            return 0

        lax.fori_loop(q * step, (q + 1) * step, body, 0)

    def to_plane(make):
        def body(k, _):
            make(plane_peer(me, k)).start()
            return 0

        lax.fori_loop(1, Z, body, 0)

    def scatter_sums(w):
        to_plane(lambda t: pltpu.make_async_remote_copy(
            src_ref=sums.at[w, t], dst_ref=parts.at[w, me], send_sem=rs_send.at[w], recv_sem=rs_recv.at[w],
            device_id={"zero": t}, device_id_type=MESH))
        parts[w, me] = sums[w, me]

    def gather_scales(w):
        got = parts.at[w, pl.ds(0, Z - 1)]
        pltpu.make_async_copy(got, got, rs_recv.at[w]).wait()
        scales[w, me] = jnp.sqrt(jnp.sum(parts[w], axis=0))
        to_plane(lambda t: pltpu.make_async_remote_copy(
            src_ref=scales.at[w, me], dst_ref=scales.at[w, me], send_sem=ag_send.at[w], recv_sem=ag_recv.at[w],
            device_id={"zero": t}, device_id_type=MESH))

    def finish_scales(w):
        got = scales.at[w, pl.ds(0, Z - 1)]
        pltpu.make_async_copy(got, got, ag_recv.at[w]).wait()
        inverse[w] = 1.0 / scales[w]

    def narrow(w, p):
        e0 = 2 * p + core
        e1 = 2 * p + 1 - core
        for h in range(2):
            turned = []
            for b in range(h * half, (h + 1) * half):
                at = slice(b * LANES, (b + 1) * LANES)
                x0 = held[w, e0, :, at] * inverse[w, e0, b:b + 1, :]
                x1 = held[w, e1, :, at] * inverse[w, e1, b:b + 1, :]
                turned.append(jnp.concatenate([x0, x1], axis=0).T)
            t = jnp.concatenate(turned, axis=0).reshape(Z // 2, own, LANES).astype(jnp.bfloat16)
            send[pl.ds(h * (Z // 2), Z // 2), w * pairs + p] = t

    def send_chunk(ch):
        at = pl.ds(ch * chunk, chunk)
        to_plane(lambda t: pltpu.make_async_remote_copy(
            src_ref=send.at[t, at], dst_ref=recv.at[me, at], send_sem=bulk_send, recv_sem=bulk_recv.at[ch],
            device_id={"zero": t}, device_id_type=MESH))
        recv[me, at] = send[me, at]

    for q in range(loads):
        sums_of(0, q)
    pl.semaphore_wait(barrier, Z - 1 + 6)
    scatter_sums(0)
    for q in range(loads):
        sums_of(1, q)
    scatter_sums(1)

    def router_row(k, _):
        t = (((me // 8 + k // 4) % 4) * 4 + (me // 2 + k) % 4) * 2 + core
        pltpu.make_async_remote_copy(
            src_ref=router_part.at[me // 2], dst_ref=router_part.at[me // 2],
            send_sem=rt_send, recv_sem=rt_recv, device_id={"zero": t}, device_id_type=MESH).start()
        return 0

    gather_scales(0)
    gather_scales(1)
    lax.fori_loop(1, 16, router_row, 0)

    per_weight = pairs // chunk
    for w in range(2):
        finish_scales(w)

        def out(i, _):
            def one(p, _):
                narrow(w, p)
                return 0

            lax.fori_loop(i * chunk, (i + 1) * chunk, one, 0)
            send_chunk(w * per_weight + i)
            return 0

        lax.fori_loop(0, per_weight, out, 0)

    got = router_part.at[pl.ds(0, 15)]
    pltpu.make_async_copy(got, got, rt_recv).wait()
    router_got[2 * bank + core] = router_part[...]
    for dz in range(4):
        for dc in range(2):
            if dz or dc:
                pltpu.make_async_remote_copy(
                    src_ref=router_part, dst_ref=router_got.at[2 * bank + core], send_sem=rx_send, recv_sem=rx_recv,
                    device_id={"bank": (bank + dz) % 4, "zero": (me // 2) * 2 + (core + dc) % 2},
                    device_id_type=MESH).start()

    for w, o in ((0, out_sgate), (1, out_sup)):
        for b in range(blocks):
            scales_t[b * LANES:(b + 1) * LANES, :] = scales[w, :, b, :].T
        o[...] = scales_t[pl.ds(pl.multiple_of(me * own, 8), own), :]

    low_lanes = lax.broadcasted_iota(jnp.int32, (own, LANES), 1) < LANES // 2

    def join(ch):
        at = pl.ds(ch * chunk, chunk)
        got = recv.at[pl.ds(0, Z - 1), at]
        pltpu.make_async_copy(got, got, bulk_recv.at[ch]).wait()

    def merge(out, g, p):
        for k in range(Z // 2):
            a = recv[2 * k, g].astype(jnp.float32)
            b = recv[2 * k + 1, g].astype(jnp.float32)
            at = slice(k * LANES, (k + 1) * LANES)
            out[2 * p, :, at] = jnp.where(low_lanes, a, b).astype(jnp.bfloat16)
            out[2 * p + 1, :, at] = pltpu.roll(jnp.where(low_lanes, b, a), LANES // 2, 1).astype(jnp.bfloat16)

    def take(w, out):
        def body(i, _):
            join(w * per_weight + i)

            def one(p, _):
                merge(out, w * pairs + p, p)
                return 0

            lax.fori_loop(i * chunk, (i + 1) * chunk, one, 0)
            return 0

        lax.fori_loop(0, per_weight, body, 0)

    take(0, out_gate)

    got = router_got.at[pl.ds(0, 7)]
    pltpu.make_async_copy(got, got, rx_recv).wait()
    low_r = lax.broadcasted_iota(jnp.int32, (16, LANES), 1) < LANES // 2

    def router_rows(k, _):
        pieces = []
        for z in range(4):
            a = router_got[2 * z, k].astype(jnp.float32)
            b = router_got[2 * z + 1, k].astype(jnp.float32)
            pieces.append(jnp.where(low_r, a, b))
            pieces.append(pltpu.roll(jnp.where(low_r, b, a), LANES // 2, 1))
        out_router[pl.ds(pl.multiple_of(k * LANES, LANES), LANES), :] = (
            jnp.concatenate(pieces, axis=0).T.astype(jnp.bfloat16))
        return 0

    lax.fori_loop(0, 16, router_rows, 0)

    take(1, out_up)

    for w in range(2):
        left = sums.at[w, pl.ds(0, Z - 1)]
        pltpu.make_async_copy(left, left, rs_send.at[w]).wait()
        pltpu.make_async_copy(left, left, ag_send.at[w]).wait()
    left = send.at[pl.ds(0, Z - 1)]
    pltpu.make_async_copy(left, left, bulk_send).wait()
    left = router_part.at[pl.ds(0, 15)]
    pltpu.make_async_copy(left, left, rt_send).wait()
    left = router_got.at[pl.ds(0, 7)]
    pltpu.make_async_copy(left, left, rx_send).wait()


def write_out(*refs):
    n = 5
    ins, outs, sem = refs[:n], refs[n:2 * n], refs[2 * n]
    copies = []
    for i in range(n):
        copy = pltpu.make_async_copy(ins[i], outs[i], sem.at[i])
        copy.start()
        copies.append(copy)
    for copy in copies:
        copy.wait()


def shards(w_gate, w_up, router_weight, router_gain):
    experts, rows, cols = w_gate.shape
    own = cols // Z
    chunk = 4
    pairs = experts // 2
    chunks = 2 * pairs // chunk
    f32, bf16 = jnp.float32, jnp.bfloat16
    dma = pltpu.SemaphoreType.DMA
    hbm = pl.BlockSpec(memory_space=pltpu.HBM)
    vmem = pl.BlockSpec(memory_space=pltpu.VMEM)
    shapes = [
        ((experts, own, Z * rows), bf16), ((experts, own, Z * rows), bf16),
        ((own, experts), f32), ((own, experts), f32), ((Z * rows, LANES), bf16),
    ]
    moved = pl.pallas_call(
        functools.partial(exchange, experts, rows, cols, chunk),
        out_shape=[pltpu.VMEM(s, d) for s, d in shapes],
        in_specs=[hbm, hbm, vmem, vmem],
        out_specs=[vmem] * 5,
        scratch_shapes=[
            pltpu.VMEM((2, experts, rows, cols), f32),
            pltpu.VMEM((2, experts, cols // LANES, LANES), f32),
            pltpu.VMEM((2, Z, cols // LANES, LANES), f32),
            pltpu.VMEM((2, experts, cols // LANES, LANES), f32),
            pltpu.VMEM((2, experts, cols // LANES, LANES), f32),
            pltpu.VMEM((cols, experts), f32),
            pltpu.VMEM((Z, 2 * pairs, own, LANES), bf16),
            pltpu.VMEM((Z, 2 * pairs, own, LANES), bf16),
            pltpu.VMEM((16, 16, LANES), bf16),
            pltpu.VMEM((8, 16, 16, LANES), bf16),
            dma((8,)), dma((2,)), dma((2,)), dma((2,)), dma((2,)), dma, dma((chunks,)),
            dma, dma, dma, dma,
        ],
        compiler_params=pltpu.CompilerParams(
            collective_id=0, has_side_effects=True, vmem_limit_bytes=54 << 20),
    )(w_gate, w_up, router_weight.T, router_gain[None, :])
    outs = pl.pallas_call(
        write_out,
        out_shape=[jax.ShapeDtypeStruct(s, d) for s, d in shapes],
        in_specs=[pl.BlockSpec(memory_space=pl.ANY)] * 5,
        out_specs=[hbm] * 5,
        scratch_shapes=[dma((5,))],
        compiler_params=pltpu.CompilerParams(vmem_limit_bytes=1 << 20),
    )(*moved)
    gate, up, sgate, sup, router = outs
    return (gate.transpose(0, 2, 1), up.transpose(0, 2, 1), sgate.T, sup.T, router)


def solution(mesh):
    placed = (P("bank", "zero", None), P("bank", "zero", None), P("zero", "bank"), P("zero"))
    return jax.shard_map(
        shards,
        mesh=mesh,
        in_specs=placed,
        out_specs=(
            P("bank", None, "zero"),
            P("bank", None, "zero"),
            P("bank", "zero"),
            P("bank", "zero"),
            P(),
        ),
        check_vma=False,
    )
```

time: 309 us -> 95.7 us (0.31); the launches traced: 302 us -> 95.5 us
  local copies, waits for them, and re-layouts: 122 us -> 0 us
  waiting for transfers between devices: 119 us -> 0 us
  Pallas kernels: 0 us -> 94.9 us
  other arithmetic: 28.2 us -> 0 us
  starting transfers between devices: 19 us -> 0 us
  between operations: 14.2 us -> 0.64 us
    pallas_call x0 -> x2, Pallas kernels: none -> 94.9 us  [the longest x1 91.9 us: shards(): pl.pallas_call(functools.partial(exchange, experts, rows, cols, chunk), o...]
    unnamed x14 -> x0, local copies, waits for them, and re-layouts: 76.5 us -> none
    all_to_all x3 -> x0, waiting for transfers between devices: 70.8 us -> none  [the longest x1 70.8 us: in_one_piece(): lax.all_to_all(both, axis, split_axis=split_dim, concat_axis=concat_dim,...]
    all_gather x2 -> x0, waiting for transfers between devices: 47.7 us -> none  [over_pieces(): return lax.all_gather(value, axis).sum(0)]
    slice x5 -> x0, local copies, waits for them, and re-layouts: 34.8 us -> none  [in_one_piece(): outs.append(lax.slice_in_dim(filled, at, at + a.shape[along], axis=along))]
    all_to_all x3 -> x0, starting transfers between devices: 19 us -> none  [the longest x2 13.6 us: from_everyone(): lax.all_to_all(jnp.broadcast_to(value[None], (count, *value.shape)), axis...]
    reduce_sum x4 -> x0, other arithmetic: 12.4 us -> none  [the longest x1 4.15 us: shards(): jnp.sum(w_gate * w_gate, axis=1)]
    all_to_all x2 -> x0, local copies, waits for them, and re-layouts: 9.61 us -> none  [the longest x1 9.5 us: in_one_piece(): lax.all_to_all(both, axis, split_axis=split_dim, concat_axis=concat_dim,...]
  transfers between devices with their start and end apart: 5 -> 0, of which waited for: 3 -> 0; matrix products, arithmetic and copies ran while one was open for 26% -> 0% of each run, Pallas kernels for 0% -> 0%
where the time goes in v1:
time: 95.7 us; the launch traced here: 95.5 us
  Pallas kernels  94.9 us (99%)
    pallas_call x1, Pallas kernels, shards(): pl.pallas_call(functools.partial(exchange, experts, rows, cols, chunk), o...  91.9 us
    pallas_call x1, Pallas kernels, shards(): pl.pallas_call(write_out, out_shape=[jax.ShapeDtypeStruct(s, d) for s, d...  2.92 us

profile of v1, /device:TPU:1, one launch (start us, length us, event | category | flops | bytes accessed | tf_op | source)
XLA Modules:
  0.0 95.5 jit_solution(10205926165599377332)
XLA Ops:
  0.6 91.9 %shard_map.83 = (bf16[32,24,2048]{2,1,0:T(8,128)(2,1)S(1)}, bf16[32,24,2048]{2,1,0:T(8,128)(2,1)S(1)}, f32[24,32]{1,0:T(8,128)S(1)}, f32[24,32]{1,0:T(8,128)S(1)}, bf16[2048,128]{1,0:T(8,128)(2,1)S(1)}) custom-call(f32[32,64,768]{2,1,0:T(8,128)} %gate_hbm.1, f32[32,64,768]{2,1,0:T(8,128)} %up_hbm.1, f32[32,64]{1,0:T(8,128)} %bitcast.6, f32[1,64]{1,0:T(1,128)} %bitcast.7), custom_call_target="tpu_custom_call" | custom-call | tf_op jit(solution)/shard_map/pallas_call | solution.py:265
  92.6 2.9 %shard_map.84 = (bf16[32,24,2048]{2,1,0:T(8,128)(2,1)}, bf16[32,24,2048]{2,1,0:T(8,128)(2,1)}, f32[24,32]{1,0:T(8,128)}, f32[24,32]{1,0:T(8,128)}, bf16[2048,128]{1,0:T(8,128)(2,1)}) custom-call(bf16[32,24,2048]{2,1,0:T(8,128)(2,1)S(1)} %get-tuple-element.15.refs_0_, bf16[32,24,2048]{2,1,0:T(8,128)(2,1)S(1)} %get-tuple-element.16.refs_1_, ...), custom_call_target="tpu_custom_call" | custom-call | tf_op jit(solution)/shard_map/pallas_call | solution.py:287

commit v2 on v1

--- a/solution.py
+++ b/solution.py
@@ -12,6 +12,17 @@
 LANES = 128
 
 
+STEPS = sorted(
+    ((dy, dx, dc) for dy in range(4) for dx in range(4) for dc in range(2) if dy or dx or dc),
+    key=lambda s: -(min(s[0], 4 - s[0]) + min(s[1], 4 - s[1])),
+)
+
+
+def stepped(me, step):
+    y, x, c = me // 8, (me // 2) % 4, me % 2
+    return (((y + step[0]) % 4) * 4 + (x + step[1]) % 4) * 2 + (c + step[2]) % 2
+
+
 def plane_peer(me, k):
     k = (11 * k) % 32
     dy, dx, dc = k // 8, (k // 2) % 4, k % 2
@@ -20,11 +31,12 @@
 
 
 def exchange(
-    experts, rows, cols, chunk,
-    gate_hbm, up_hbm, router_ref, gain_ref,
+    experts, rows, cols, raw, chunk,
+    gate_hbm, up_hbm, router_hbm, gain_hbm,
     out_gate, out_up, out_sgate, out_sup, out_router,
-    held, sums, parts, scales, inverse, scales_t, send, recv, router_part, router_got,
-    load_sem, rs_send, rs_recv, ag_send, ag_recv, bulk_send, bulk_recv,
+    held, sums, parts, scales, inverse, scales_t, send, recv, raw_send, raw_recv, router_ref, gain_ref, router_part, router_got,
+    small_sem, load_sem, rs_send, rs_recv, ag_send, ag_recv, bulk_sent, bulk_got,
+    raw_sent, raw_got,
     rt_send, rt_recv, rx_send, rx_recv,
 ):
     bank = lax.axis_index("bank")
@@ -38,6 +50,19 @@
     loads = 4
     step = experts // loads
 
+    def load(w, q):
+        at = pl.ds(q * step, step)
+        return pltpu.make_async_copy(weights[w].at[at], held.at[w, at], load_sem.at[w * loads + q])
+
+    for q in range(loads):
+        load(0, q).start()
+    small = [
+        pltpu.make_async_copy(router_hbm, router_ref, small_sem.at[0]),
+        pltpu.make_async_copy(gain_hbm, gain_ref, small_sem.at[1]),
+    ]
+    for copy in small:
+        copy.start()
+
     barrier = pltpu.get_barrier_semaphore()
 
     def greet(k, _):
@@ -53,23 +78,8 @@
                 device_id_type=MESH,
             )
 
-    copies = []
-    for w in range(2):
-        for q in range(loads):
-            at = pl.ds(q * step, step)
-            copy = pltpu.make_async_copy(weights[w].at[at], held.at[w, at], load_sem.at[w * loads + q])
-            copy.start()
-            copies.append(copy)
-
-    low = router_ref[:16, :] * gain_ref[...]
-    high = router_ref[16:, :] * gain_ref[...]
-    first = jnp.where(core == 0, low, high)
-    second = jnp.where(core == 0, high, low)
-    packed = jnp.concatenate([first, second], axis=1).astype(jnp.bfloat16)
-    router_part[me // 2] = packed
-
     def sums_of(w, q):
-        copies[w * loads + q].wait()
+        load(w, q).wait()
 
         def body(e, _):
             for b in range(blocks):
@@ -80,11 +90,8 @@
         lax.fori_loop(q * step, (q + 1) * step, body, 0)
 
     def to_plane(make):
-        def body(k, _):
-            make(plane_peer(me, k)).start()
-            return 0
-
-        lax.fori_loop(1, Z, body, 0)
+        for s in STEPS:
+            make(stepped(me, s)).start()
 
     def scatter_sums(w):
         to_plane(lambda t: pltpu.make_async_remote_copy(
@@ -105,33 +112,64 @@
         pltpu.make_async_copy(got, got, ag_recv.at[w]).wait()
         inverse[w] = 1.0 / scales[w]
 
-    def narrow(w, p):
-        e0 = 2 * p + core
-        e1 = 2 * p + 1 - core
+    def turn(p, piece):
         for h in range(2):
             turned = []
             for b in range(h * half, (h + 1) * half):
-                at = slice(b * LANES, (b + 1) * LANES)
-                x0 = held[w, e0, :, at] * inverse[w, e0, b:b + 1, :]
-                x1 = held[w, e1, :, at] * inverse[w, e1, b:b + 1, :]
-                turned.append(jnp.concatenate([x0, x1], axis=0).T)
-            t = jnp.concatenate(turned, axis=0).reshape(Z // 2, own, LANES).astype(jnp.bfloat16)
-            send[pl.ds(h * (Z // 2), Z // 2), w * pairs + p] = t
-
-    def send_chunk(ch):
-        at = pl.ds(ch * chunk, chunk)
+                both = [piece(e, b) for e in (2 * p + core, 2 * p + 1 - core)]
+                turned.append(jnp.concatenate(both, axis=0).T)
+            yield h, jnp.concatenate(turned, axis=0).reshape(Z // 2, own, LANES)
+
+    def narrow(w, p):
+        def piece(e, b):
+            return held[w, e, :, b * LANES:(b + 1) * LANES] * inverse[w, e, b:b + 1, :]
+
+        for h, t in turn(p, piece):
+            send[pl.ds(h * (Z // 2), Z // 2), w * pairs + p] = t.astype(jnp.bfloat16)
+
+    def copy_raw(p):
+        for h, t in turn(p, lambda e, b: held[0, e, :, b * LANES:(b + 1) * LANES]):
+            raw_send[p, pl.ds(h * (Z // 2), Z // 2)] = t
+
+    def send_raw(p):
         to_plane(lambda t: pltpu.make_async_remote_copy(
-            src_ref=send.at[t, at], dst_ref=recv.at[me, at], send_sem=bulk_send, recv_sem=bulk_recv.at[ch],
+            src_ref=raw_send.at[p, t], dst_ref=raw_recv.at[p, me], send_sem=raw_sent.at[p], recv_sem=raw_got.at[p],
             device_id={"zero": t}, device_id_type=MESH))
+        raw_recv[p, me] = raw_send[p, me]
+
+    first_pair = (raw, 0)
+    base = (0, (pairs - raw) // chunk[0])
+
+    def span(w, i):
+        return first_pair[w] + i * chunk[w]
+
+    def count(w):
+        return (pairs - first_pair[w]) // chunk[w]
+
+    def send_chunk(w, i):
+        at = pl.ds(w * pairs + span(w, i), chunk[w])
+        for s in STEPS:
+            t = stepped(me, s)
+            pltpu.make_async_remote_copy(
+                src_ref=send.at[t, at], dst_ref=recv.at[me, at], send_sem=bulk_sent, recv_sem=bulk_got.at[base[w] + i],
+                device_id={"zero": t}, device_id_type=MESH).start()
         recv[me, at] = send[me, at]
 
     for q in range(loads):
+        load(1, q).start()
         sums_of(0, q)
+    for p in range(raw):
+        copy_raw(p)
     pl.semaphore_wait(barrier, Z - 1 + 6)
     scatter_sums(0)
-    for q in range(loads):
-        sums_of(1, q)
-    scatter_sums(1)
+
+    for copy in small:
+        copy.wait()
+    low = router_ref[:16, :] * gain_ref[...]
+    high = router_ref[16:, :] * gain_ref[...]
+    first = jnp.where(core == 0, low, high)
+    second = jnp.where(core == 0, high, low)
+    router_part[me // 2] = jnp.concatenate([first, second], axis=1).astype(jnp.bfloat16)
 
     def router_row(k, _):
         t = (((me // 8 + k // 4) % 4) * 4 + (me // 2 + k) % 4) * 2 + core
@@ -140,24 +178,26 @@
             send_sem=rt_send, recv_sem=rt_recv, device_id={"zero": t}, device_id_type=MESH).start()
         return 0
 
+    lax.fori_loop(1, 16, router_row, 0)
+
+    for q in range(loads):
+        sums_of(1, q)
+    scatter_sums(1)
     gather_scales(0)
+    for p in range(raw):
+        send_raw(p)
     gather_scales(1)
-    lax.fori_loop(1, 16, router_row, 0)
-
-    per_weight = pairs // chunk
+
     for w in range(2):
         finish_scales(w)
 
         def out(i, _):
-            def one(p, _):
-                narrow(w, p)
-                return 0
-
-            lax.fori_loop(i * chunk, (i + 1) * chunk, one, 0)
-            send_chunk(w * per_weight + i)
+            for j in range(chunk[w]):
+                narrow(w, span(w, i) + j)
+            send_chunk(w, i)
             return 0
 
-        lax.fori_loop(0, per_weight, out, 0)
+        lax.fori_loop(0, count(w), out, 0)
 
     got = router_part.at[pl.ds(0, 15)]
     pltpu.make_async_copy(got, got, rt_recv).wait()
@@ -177,11 +217,6 @@
 
     low_lanes = lax.broadcasted_iota(jnp.int32, (own, LANES), 1) < LANES // 2
 
-    def join(ch):
-        at = pl.ds(ch * chunk, chunk)
-        got = recv.at[pl.ds(0, Z - 1), at]
-        pltpu.make_async_copy(got, got, bulk_recv.at[ch]).wait()
-
     def merge(out, g, p):
         for k in range(Z // 2):
             a = recv[2 * k, g].astype(jnp.float32)
@@ -192,16 +227,26 @@
 
     def take(w, out):
         def body(i, _):
-            join(w * per_weight + i)
-
-            def one(p, _):
-                merge(out, w * pairs + p, p)
-                return 0
-
-            lax.fori_loop(i * chunk, (i + 1) * chunk, one, 0)
+            got = recv.at[pl.ds(0, Z - 1), pl.ds(w * pairs + span(w, i), chunk[w])]
+            pltpu.make_async_copy(got, got, bulk_got.at[base[w] + i]).wait()
+            for j in range(chunk[w]):
+                merge(out, w * pairs + span(w, i) + j, span(w, i) + j)
             return 0
 
-        lax.fori_loop(0, per_weight, body, 0)
+        lax.fori_loop(0, count(w), body, 0)
+
+    for p in range(raw):
+        got = raw_recv.at[p, pl.ds(0, Z - 1)]
+        pltpu.make_async_copy(got, got, raw_got.at[p]).wait()
+        even = 1.0 / out_sgate[:, 2 * p:2 * p + 1]
+        odd = 1.0 / out_sgate[:, 2 * p + 1:2 * p + 2]
+        for k in range(Z // 2):
+            a = raw_recv[p, 2 * k]
+            b = raw_recv[p, 2 * k + 1]
+            at = slice(k * LANES, (k + 1) * LANES)
+            out_gate[2 * p, :, at] = (jnp.where(low_lanes, a, b) * even).astype(jnp.bfloat16)
+            out_gate[2 * p + 1, :, at] = (
+                pltpu.roll(jnp.where(low_lanes, b, a), LANES // 2, 1) * odd).astype(jnp.bfloat16)
 
     take(0, out_gate)
 
@@ -228,8 +273,11 @@
         left = sums.at[w, pl.ds(0, Z - 1)]
         pltpu.make_async_copy(left, left, rs_send.at[w]).wait()
         pltpu.make_async_copy(left, left, ag_send.at[w]).wait()
-    left = send.at[pl.ds(0, Z - 1)]
-    pltpu.make_async_copy(left, left, bulk_send).wait()
+    for p in range(raw):
+        left = raw_send.at[p, pl.ds(0, Z - 1)]
+        pltpu.make_async_copy(left, left, raw_sent.at[p]).wait()
+    left = send.at[pl.ds(0, Z - 1), pl.ds(raw, 2 * pairs - raw)]
+    pltpu.make_async_copy(left, left, bulk_sent).wait()
     left = router_part.at[pl.ds(0, 15)]
     pltpu.make_async_copy(left, left, rt_send).wait()
     left = router_got.at[pl.ds(0, 7)]
@@ -251,9 +299,10 @@
 def shards(w_gate, w_up, router_weight, router_gain):
     experts, rows, cols = w_gate.shape
     own = cols // Z
-    chunk = 4
+    raw = 1
+    chunk = (1, 1)
     pairs = experts // 2
-    chunks = 2 * pairs // chunk
+    chunks = (pairs - raw) // chunk[0] + pairs // chunk[1]
     f32, bf16 = jnp.float32, jnp.bfloat16
     dma = pltpu.SemaphoreType.DMA
     hbm = pl.BlockSpec(memory_space=pltpu.HBM)
@@ -263,9 +312,9 @@
         ((own, experts), f32), ((own, experts), f32), ((Z * rows, LANES), bf16),
     ]
     moved = pl.pallas_call(
-        functools.partial(exchange, experts, rows, cols, chunk),
+        functools.partial(exchange, experts, rows, cols, raw, chunk),
         out_shape=[pltpu.VMEM(s, d) for s, d in shapes],
-        in_specs=[hbm, hbm, vmem, vmem],
+        in_specs=[hbm] * 4,
         out_specs=[vmem] * 5,
         scratch_shapes=[
             pltpu.VMEM((2, experts, rows, cols), f32),
@@ -276,9 +325,14 @@
             pltpu.VMEM((cols, experts), f32),
             pltpu.VMEM((Z, 2 * pairs, own, LANES), bf16),
             pltpu.VMEM((Z, 2 * pairs, own, LANES), bf16),
+            pltpu.VMEM((raw, Z, own, LANES), f32),
+            pltpu.VMEM((raw, Z, own, LANES), f32),
+            pltpu.VMEM((experts, rows), f32),
+            pltpu.VMEM((1, rows), f32),
             pltpu.VMEM((16, 16, LANES), bf16),
             pltpu.VMEM((8, 16, 16, LANES), bf16),
-            dma((8,)), dma((2,)), dma((2,)), dma((2,)), dma((2,)), dma, dma((chunks,)),
+            dma((2,)), dma((8,)), dma((2,)), dma((2,)), dma((2,)), dma((2,)), dma, dma((chunks,)),
+            dma((raw,)), dma((raw,)),
             dma, dma, dma, dma,
         ],
         compiler_params=pltpu.CompilerParams(

time: 95.7 us -> 92.2 us (0.963)
  Pallas kernels: 94.9 us -> 91.4 us
    pallas_call x1, Pallas kernels: 91.9 us -> 88.5 us  [shards(): pl.pallas_call(functools.partial(exchange, experts, rows, cols, raw, chun...]
where the time goes in v2:
time: 92.2 us; the launch traced here: 92.1 us
  Pallas kernels  91.4 us (99%)
    pallas_call x1, Pallas kernels, shards(): pl.pallas_call(functools.partial(exchange, experts, rows, cols, raw, chun...  88.5 us
    pallas_call x1, Pallas kernels, shards(): pl.pallas_call(write_out, out_shape=[jax.ShapeDtypeStruct(s, d) for s, d...  2.92 us

profile of v2, /device:TPU:1, one launch (start us, length us, event | category | flops | bytes accessed | tf_op | source)
XLA Modules:
  0.0 92.1 jit_solution(4900362975912984601)
XLA Ops:
  0.6 88.5 %shard_map.83 = (bf16[32,24,2048]{2,1,0:T(8,128)(2,1)S(1)}, bf16[32,24,2048]{2,1,0:T(8,128)(2,1)S(1)}, f32[24,32]{1,0:T(8,128)S(1)}, f32[24,32]{1,0:T(8,128)S(1)}, bf16[2048,128]{1,0:T(8,128)(2,1)S(1)}) custom-call(f32[32,64,768]{2,1,0:T(8,128)} %gate_hbm.1, f32[32,64,768]{2,1,0:T(8,128)} %up_hbm.1, f32[32,64]{1,0:T(8,128)} %bitcast.6, f32[1,64]{1,0:T(1,128)} %bitcast.7), custom_call_target="tpu_custom_call" | custom-call | tf_op jit(solution)/shard_map/pallas_call | solution.py:314
  89.2 2.9 %shard_map.84 = (bf16[32,24,2048]{2,1,0:T(8,128)(2,1)}, bf16[32,24,2048]{2,1,0:T(8,128)(2,1)}, f32[24,32]{1,0:T(8,128)}, f32[24,32]{1,0:T(8,128)}, bf16[2048,128]{1,0:T(8,128)(2,1)}) custom-call(bf16[32,24,2048]{2,1,0:T(8,128)(2,1)S(1)} %get-tuple-element.15.refs_0_, bf16[32,24,2048]{2,1,0:T(8,128)(2,1)S(1)} %get-tuple-element.16.refs_1_, ...), custom_call_target="tpu_custom_call" | custom-call | tf_op jit(solution)/shard_map/pallas_call | solution.py:341

commit v3 on v2

--- a/solution.py
+++ b/solution.py
@@ -18,25 +18,21 @@
 )
 
 
+FAR = 22
+
+
 def stepped(me, step):
     y, x, c = me // 8, (me // 2) % 4, me % 2
     return (((y + step[0]) % 4) * 4 + (x + step[1]) % 4) * 2 + (c + step[2]) % 2
 
 
-def plane_peer(me, k):
-    k = (11 * k) % 32
-    dy, dx, dc = k // 8, (k // 2) % 4, k % 2
-    y, x, c = me // 8, (me // 2) % 4, me % 2
-    return (((y + dy) % 4) * 4 + (x + dx) % 4) * 2 + (c + dc) % 2
-
-
 def exchange(
-    experts, rows, cols, raw, chunk,
+    experts, rows, cols, tiles, chunk,
     gate_hbm, up_hbm, router_hbm, gain_hbm,
     out_gate, out_up, out_sgate, out_sup, out_router,
     held, sums, parts, scales, inverse, scales_t, send, recv, raw_send, raw_recv, router_ref, gain_ref, router_part, router_got,
     small_sem, load_sem, rs_send, rs_recv, ag_send, ag_recv, bulk_sent, bulk_got,
-    raw_sent, raw_got,
+    raw_sent, raw_got, rest_sent, rest_got,
     rt_send, rt_recv, rx_send, rx_recv,
 ):
     bank = lax.axis_index("bank")
@@ -46,6 +42,9 @@
     own = cols // Z
     pairs = experts // 2
     half = blocks // 2
+    per_pair = own // 8
+    raw = -(-sum(tiles) // per_pair)
+    kept = own - 8 * (sum(tiles) - (raw - 1) * per_pair)
     weights = (gate_hbm, up_hbm)
     loads = 4
     step = experts // loads
@@ -53,6 +52,13 @@
     def load(w, q):
         at = pl.ds(q * step, step)
         return pltpu.make_async_copy(weights[w].at[at], held.at[w, at], load_sem.at[w * loads + q])
+
+    barrier = pltpu.get_barrier_semaphore()
+    for s in STEPS:
+        pl.semaphore_signal(barrier, inc=1, device_id={"zero": stepped(me, s)}, device_id_type=MESH)
+    up_bank, down_bank = (bank + 1) % 4, (bank + 3) % 4
+    for other in (up_bank, down_bank):
+        pl.semaphore_signal(barrier, inc=1, device_id={"bank": other}, device_id_type=MESH)
 
     for q in range(loads):
         load(0, q).start()
@@ -63,21 +69,6 @@
     for copy in small:
         copy.start()
 
-    barrier = pltpu.get_barrier_semaphore()
-
-    def greet(k, _):
-        pl.semaphore_signal(barrier, inc=1, device_id={"zero": plane_peer(me, k)}, device_id_type=MESH)
-        return 0
-
-    lax.fori_loop(1, Z, greet, 0)
-    for dz in range(1, 4):
-        for dc in range(2):
-            pl.semaphore_signal(
-                barrier, inc=1,
-                device_id={"bank": (bank + dz) % 4, "zero": (me // 2) * 2 + (core + dc) % 2},
-                device_id_type=MESH,
-            )
-
     def sums_of(w, q):
         load(w, q).wait()
 
@@ -131,11 +122,13 @@
         for h, t in turn(p, lambda e, b: held[0, e, :, b * LANES:(b + 1) * LANES]):
             raw_send[p, pl.ds(h * (Z // 2), Z // 2)] = t
 
-    def send_raw(p):
+    def send_raw(i):
+        p, at = i // per_pair, pl.ds(8 * (i % per_pair), 8)
         to_plane(lambda t: pltpu.make_async_remote_copy(
-            src_ref=raw_send.at[p, t], dst_ref=raw_recv.at[p, me], send_sem=raw_sent.at[p], recv_sem=raw_got.at[p],
+            src_ref=raw_send.at[p, t, at], dst_ref=raw_recv.at[p, me, at],
+            send_sem=raw_sent.at[i], recv_sem=raw_got.at[i],
             device_id={"zero": t}, device_id_type=MESH))
-        raw_recv[p, me] = raw_send[p, me]
+        raw_recv[p, me, at] = raw_send[p, me, at]
 
     first_pair = (raw, 0)
     base = (0, (pairs - raw) // chunk[0])
@@ -146,13 +139,18 @@
     def count(w):
         return (pairs - first_pair[w]) // chunk[w]
 
-    def send_chunk(w, i):
+    def send_chunk(w, i, steps):
         at = pl.ds(w * pairs + span(w, i), chunk[w])
-        for s in STEPS:
+        for s in steps:
             t = stepped(me, s)
             pltpu.make_async_remote_copy(
                 src_ref=send.at[t, at], dst_ref=recv.at[me, at], send_sem=bulk_sent, recv_sem=bulk_got.at[base[w] + i],
                 device_id={"zero": t}, device_id_type=MESH).start()
+
+    def prepare(w, i):
+        for j in range(chunk[w]):
+            narrow(w, span(w, i) + j)
+        at = pl.ds(w * pairs + span(w, i), chunk[w])
         recv[me, at] = send[me, at]
 
     for q in range(loads):
@@ -160,7 +158,7 @@
         sums_of(0, q)
     for p in range(raw):
         copy_raw(p)
-    pl.semaphore_wait(barrier, Z - 1 + 6)
+    pl.semaphore_wait(barrier, Z - 1 + 2)
     scatter_sums(0)
 
     for copy in small:
@@ -179,36 +177,81 @@
         return 0
 
     lax.fori_loop(1, 16, router_row, 0)
-
+    for i in range(tiles[0]):
+        send_raw(i)
     for q in range(loads):
         sums_of(1, q)
     scatter_sums(1)
+    for i in range(tiles[0], tiles[0] + tiles[1]):
+        send_raw(i)
     gather_scales(0)
-    for p in range(raw):
-        send_raw(p)
+    for i in range(tiles[0] + tiles[1], sum(tiles)):
+        send_raw(i)
     gather_scales(1)
+
+    def rest(ref, t):
+        return ref.at[t, raw - 1, pl.ds(own - kept, kept)]
 
     for w in range(2):
         finish_scales(w)
-
-        def out(i, _):
-            for j in range(chunk[w]):
-                narrow(w, span(w, i) + j)
-            send_chunk(w, i)
+        if w == 0 and kept:
+            narrow(0, raw - 1)
+            to_plane(lambda t: pltpu.make_async_remote_copy(
+                src_ref=rest(send, t), dst_ref=rest(recv, me), send_sem=rest_sent, recv_sem=rest_got,
+                device_id={"zero": t}, device_id_type=MESH))
+            recv[me, raw - 1, own - kept:, :] = send[me, raw - 1, own - kept:, :]
+
+        lead = (0, 2)[w]
+
+        def begin(i, _):
+            prepare(w, i)
+            send_chunk(w, i, STEPS[:FAR])
             return 0
 
-        lax.fori_loop(0, count(w), out, 0)
+        def both(i, _):
+            begin(i + lead, 0)
+            send_chunk(w, i, STEPS[FAR:])
+            return 0
+
+        def end(i, _):
+            send_chunk(w, i, STEPS[FAR:])
+            return 0
+
+        if lead:
+            lax.fori_loop(0, lead, begin, 0)
+        lax.fori_loop(0, count(w) - lead, both, 0)
+        if lead:
+            lax.fori_loop(count(w) - lead, count(w), end, 0)
+
+    partner = {"zero": (me // 2) * 2 + 1 - core}
+    opposite = (bank + 2) % 4
+
+    def pass_on(of_bank, to, sem):
+        slot = router_got.at[2 * of_bank + core]
+        pltpu.make_async_remote_copy(
+            src_ref=slot, dst_ref=slot, send_sem=rx_send.at[sem], recv_sem=rx_recv.at[sem],
+            device_id=to, device_id_type=MESH).start()
+
+    def passed_on(count, sem, which):
+        got = router_got.at[pl.ds(0, count)]
+        pltpu.make_async_copy(got, got, which.at[sem]).wait()
 
     got = router_part.at[pl.ds(0, 15)]
     pltpu.make_async_copy(got, got, rt_recv).wait()
     router_got[2 * bank + core] = router_part[...]
-    for dz in range(4):
-        for dc in range(2):
-            if dz or dc:
-                pltpu.make_async_remote_copy(
-                    src_ref=router_part, dst_ref=router_got.at[2 * bank + core], send_sem=rx_send, recv_sem=rx_recv,
-                    device_id={"bank": (bank + dz) % 4, "zero": (me // 2) * 2 + (core + dc) % 2},
-                    device_id_type=MESH).start()
+    pass_on(bank, {"bank": up_bank}, 0)
+    pass_on(bank, {"bank": down_bank}, 0)
+    pass_on(bank, partner, 0)
+
+    def relay_near():
+        passed_on(3, 0, rx_recv)
+        pass_on(down_bank, {"bank": up_bank}, 1)
+        pass_on(down_bank, partner, 1)
+        pass_on(up_bank, partner, 1)
+
+    def relay_far():
+        passed_on(3, 1, rx_recv)
+        pass_on(opposite, partner, 2)
 
     for w, o in ((0, out_sgate), (1, out_sup)):
         for b in range(blocks):
@@ -225,7 +268,7 @@
             out[2 * p, :, at] = jnp.where(low_lanes, a, b).astype(jnp.bfloat16)
             out[2 * p + 1, :, at] = pltpu.roll(jnp.where(low_lanes, b, a), LANES // 2, 1).astype(jnp.bfloat16)
 
-    def take(w, out):
+    def take(w, out, start, stop):
         def body(i, _):
             got = recv.at[pl.ds(0, Z - 1), pl.ds(w * pairs + span(w, i), chunk[w])]
             pltpu.make_async_copy(got, got, bulk_got.at[base[w] + i]).wait()
@@ -233,25 +276,40 @@
                 merge(out, w * pairs + span(w, i) + j, span(w, i) + j)
             return 0
 
-        lax.fori_loop(0, count(w), body, 0)
-
+        lax.fori_loop(start, stop, body, 0)
+
+    for i in range(sum(tiles)):
+        at = pl.ds(8 * (i % per_pair), 8)
+        got = raw_recv.at[i // per_pair, pl.ds(0, Z - 1), at]
+        pltpu.make_async_copy(got, got, raw_got.at[i]).wait()
+    if kept:
+        got = rest(recv, pl.ds(0, Z - 1))
+        pltpu.make_async_copy(got, got, rest_got).wait()
     for p in range(raw):
-        got = raw_recv.at[p, pl.ds(0, Z - 1)]
-        pltpu.make_async_copy(got, got, raw_got.at[p]).wait()
         even = 1.0 / out_sgate[:, 2 * p:2 * p + 1]
         odd = 1.0 / out_sgate[:, 2 * p + 1:2 * p + 2]
         for k in range(Z // 2):
             a = raw_recv[p, 2 * k]
             b = raw_recv[p, 2 * k + 1]
             at = slice(k * LANES, (k + 1) * LANES)
-            out_gate[2 * p, :, at] = (jnp.where(low_lanes, a, b) * even).astype(jnp.bfloat16)
-            out_gate[2 * p + 1, :, at] = (
-                pltpu.roll(jnp.where(low_lanes, b, a), LANES // 2, 1) * odd).astype(jnp.bfloat16)
-
-    take(0, out_gate)
-
-    got = router_got.at[pl.ds(0, 7)]
-    pltpu.make_async_copy(got, got, rx_recv).wait()
+            one = jnp.where(low_lanes, a, b) * even
+            other = pltpu.roll(jnp.where(low_lanes, b, a), LANES // 2, 1) * odd
+            if p == raw - 1 and kept:
+                a = recv[2 * k, p].astype(jnp.float32)
+                b = recv[2 * k + 1, p].astype(jnp.float32)
+                is_raw = lax.broadcasted_iota(jnp.int32, (own, LANES), 0) < own - kept
+                one = jnp.where(is_raw, one, jnp.where(low_lanes, a, b))
+                other = jnp.where(is_raw, other, pltpu.roll(jnp.where(low_lanes, b, a), LANES // 2, 1))
+            out_gate[2 * p, :, at] = one.astype(jnp.bfloat16)
+            out_gate[2 * p + 1, :, at] = other.astype(jnp.bfloat16)
+
+    take(0, out_gate, 0, count(0) // 3)
+    relay_near()
+    take(0, out_gate, count(0) // 3, 2 * (count(0) // 3))
+    relay_far()
+    take(0, out_gate, 2 * (count(0) // 3), count(0))
+
+    passed_on(1, 2, rx_recv)
     low_r = lax.broadcasted_iota(jnp.int32, (16, LANES), 1) < LANES // 2
 
     def router_rows(k, _):
@@ -267,21 +325,24 @@
 
     lax.fori_loop(0, 16, router_rows, 0)
 
-    take(1, out_up)
+    take(1, out_up, 0, count(1))
 
     for w in range(2):
         left = sums.at[w, pl.ds(0, Z - 1)]
         pltpu.make_async_copy(left, left, rs_send.at[w]).wait()
         pltpu.make_async_copy(left, left, ag_send.at[w]).wait()
-    for p in range(raw):
-        left = raw_send.at[p, pl.ds(0, Z - 1)]
-        pltpu.make_async_copy(left, left, raw_sent.at[p]).wait()
+    for i in range(sum(tiles)):
+        left = raw_send.at[i // per_pair, pl.ds(0, Z - 1), pl.ds(8 * (i % per_pair), 8)]
+        pltpu.make_async_copy(left, left, raw_sent.at[i]).wait()
+    if kept:
+        left = rest(send, pl.ds(0, Z - 1))
+        pltpu.make_async_copy(left, left, rest_sent).wait()
     left = send.at[pl.ds(0, Z - 1), pl.ds(raw, 2 * pairs - raw)]
     pltpu.make_async_copy(left, left, bulk_sent).wait()
     left = router_part.at[pl.ds(0, 15)]
     pltpu.make_async_copy(left, left, rt_send).wait()
-    left = router_got.at[pl.ds(0, 7)]
-    pltpu.make_async_copy(left, left, rx_send).wait()
+    for sem, sent in ((0, 3), (1, 3), (2, 1)):
+        passed_on(sent, sem, rx_send)
 
 
 def write_out(*refs):
@@ -299,7 +360,8 @@
 def shards(w_gate, w_up, router_weight, router_gain):
     experts, rows, cols = w_gate.shape
     own = cols // Z
-    raw = 1
+    tiles = (1, 1, 2)
+    raw = -(-sum(tiles) // (own // 8))
     chunk = (1, 1)
     pairs = experts // 2
     chunks = (pairs - raw) // chunk[0] + pairs // chunk[1]
@@ -312,7 +374,7 @@
         ((own, experts), f32), ((own, experts), f32), ((Z * rows, LANES), bf16),
     ]
     moved = pl.pallas_call(
-        functools.partial(exchange, experts, rows, cols, raw, chunk),
+        functools.partial(exchange, experts, rows, cols, tiles, chunk),
         out_shape=[pltpu.VMEM(s, d) for s, d in shapes],
         in_specs=[hbm] * 4,
         out_specs=[vmem] * 5,
@@ -332,8 +394,8 @@
             pltpu.VMEM((16, 16, LANES), bf16),
             pltpu.VMEM((8, 16, 16, LANES), bf16),
             dma((2,)), dma((8,)), dma((2,)), dma((2,)), dma((2,)), dma((2,)), dma, dma((chunks,)),
-            dma((raw,)), dma((raw,)),
-            dma, dma, dma, dma,
+            dma((sum(tiles),)), dma((sum(tiles),)), dma, dma,
+            dma, dma, dma((3,)), dma((3,)),
         ],
         compiler_params=pltpu.CompilerParams(
             collective_id=0, has_side_effects=True, vmem_limit_bytes=54 << 20),

time: 92.2 us -> 89.9 us (0.975)
  Pallas kernels: 91.4 us -> 89.1 us
    pallas_call x1, Pallas kernels: 88.5 us -> 86.2 us  [shards(): pl.pallas_call(functools.partial(exchange, experts, rows, cols, tiles, ch...]
where the time goes in v3:
time: 89.9 us; the launch traced here: 89.8 us
  Pallas kernels  89.1 us (99%)
    pallas_call x1, Pallas kernels, shards(): pl.pallas_call(functools.partial(exchange, experts, rows, cols, tiles, ch...  86.2 us
    pallas_call x1, Pallas kernels, shards(): pl.pallas_call(write_out, out_shape=[jax.ShapeDtypeStruct(s, d) for s, d...  2.92 us

profile of v3, /device:TPU:1, one launch (start us, length us, event | category | flops | bytes accessed | tf_op | source)
XLA Modules:
  0.0 89.8 jit_solution(7555532221604344853)
XLA Ops:
  0.6 86.2 %shard_map.83 = (bf16[32,24,2048]{2,1,0:T(8,128)(2,1)S(1)}, bf16[32,24,2048]{2,1,0:T(8,128)(2,1)S(1)}, f32[24,32]{1,0:T(8,128)S(1)}, f32[24,32]{1,0:T(8,128)S(1)}, bf16[2048,128]{1,0:T(8,128)(2,1)S(1)}) custom-call(f32[32,64,768]{2,1,0:T(8,128)} %gate_hbm.1, f32[32,64,768]{2,1,0:T(8,128)} %up_hbm.1, f32[32,64]{1,0:T(8,128)} %bitcast.6, f32[1,64]{1,0:T(1,128)} %bitcast.7), custom_call_target="tpu_custom_call" | custom-call | tf_op jit(solution)/shard_map/pallas_call | solution.py:376
  86.8 2.9 %shard_map.84 = (bf16[32,24,2048]{2,1,0:T(8,128)(2,1)}, bf16[32,24,2048]{2,1,0:T(8,128)(2,1)}, f32[24,32]{1,0:T(8,128)}, f32[24,32]{1,0:T(8,128)}, bf16[2048,128]{1,0:T(8,128)(2,1)}) custom-call(bf16[32,24,2048]{2,1,0:T(8,128)(2,1)S(1)} %get-tuple-element.15.refs_0_, bf16[32,24,2048]{2,1,0:T(8,128)(2,1)S(1)} %get-tuple-element.16.refs_1_, ...), custom_call_target="tpu_custom_call" | custom-call | tf_op jit(solution)/shard_map/pallas_call | solution.py:403

commit v4 on v3

--- a/solution.py
+++ b/solution.py
@@ -14,7 +14,7 @@
 
 STEPS = sorted(
     ((dy, dx, dc) for dy in range(4) for dx in range(4) for dc in range(2) if dy or dx or dc),
-    key=lambda s: -(min(s[0], 4 - s[0]) + min(s[1], 4 - s[1])),
+    key=lambda s: (-(min(s[0], 4 - s[0]) + min(s[1], 4 - s[1])), -s[2], (s[0] - s[1]) % 4, -s[0]),
 )
 
 
@@ -362,7 +362,7 @@
     own = cols // Z
     tiles = (1, 1, 2)
     raw = -(-sum(tiles) // (own // 8))
-    chunk = (1, 1)
+    chunk = (2, 2)
     pairs = experts // 2
     chunks = (pairs - raw) // chunk[0] + pairs // chunk[1]
     f32, bf16 = jnp.float32, jnp.bfloat16

time: 89.9 us -> 89.5 us (level)
  no operation moved by 1% of the time
where the time goes in v4:
time: 89.5 us; the launch traced here: 89.4 us
  Pallas kernels  88.7 us (99%)
    pallas_call x1, Pallas kernels, shards(): pl.pallas_call(functools.partial(exchange, experts, rows, cols, tiles, ch...  85.8 us
    pallas_call x1, Pallas kernels, shards(): pl.pallas_call(write_out, out_shape=[jax.ShapeDtypeStruct(s, d) for s, d...  2.92 us

profile of v4, /device:TPU:1, one launch (start us, length us, event | category | flops | bytes accessed | tf_op | source)
XLA Modules:
  0.0 89.4 jit_solution(14558867392334994575)
XLA Ops:
  0.6 85.8 %shard_map.83 = (bf16[32,24,2048]{2,1,0:T(8,128)(2,1)S(1)}, bf16[32,24,2048]{2,1,0:T(8,128)(2,1)S(1)}, f32[24,32]{1,0:T(8,128)S(1)}, f32[24,32]{1,0:T(8,128)S(1)}, bf16[2048,128]{1,0:T(8,128)(2,1)S(1)}) custom-call(f32[32,64,768]{2,1,0:T(8,128)} %gate_hbm.1, f32[32,64,768]{2,1,0:T(8,128)} %up_hbm.1, f32[32,64]{1,0:T(8,128)} %bitcast.6, f32[1,64]{1,0:T(1,128)} %bitcast.7), custom_call_target="tpu_custom_call" | custom-call | tf_op jit(solution)/shard_map/pallas_call | solution.py:376
  86.5 2.9 %shard_map.84 = (bf16[32,24,2048]{2,1,0:T(8,128)(2,1)}, bf16[32,24,2048]{2,1,0:T(8,128)(2,1)}, f32[24,32]{1,0:T(8,128)}, f32[24,32]{1,0:T(8,128)}, bf16[2048,128]{1,0:T(8,128)(2,1)}) custom-call(bf16[32,24,2048]{2,1,0:T(8,128)(2,1)S(1)} %get-tuple-element.15.refs_0_, bf16[32,24,2048]{2,1,0:T(8,128)(2,1)S(1)} %get-tuple-element.16.refs_1_, ...), custom_call_target="tpu_custom_call" | custom-call | tf_op jit(solution)/shard_map/pallas_call | solution.py:403
